TPU v7x, 32 devices: a whole 2x2x4 slice. The times are simulated.
32 devices in a mesh: groups: 2 (over y), seq: 4 (over z), head: 2 (over x), dim: 2 (over core).
Axes of the slice: x: 2, y: 2, z: 4, core: 2. Of those that a mesh axis runs over, the one named last changes fastest.
Arguments:
- query: bfloat16 [4, 16, 1024, 128], P('groups', 'head', 'seq'), parts along dimension 0, may hold values from -6 to 6
- key: bfloat16 [4, 16, 1024, 128], P('groups', 'head', 'seq'), parts along dimension 0, may hold values from -6 to 6
- value: bfloat16 [4, 16, 128, 1024], P('groups', 'head', 'dim', 'seq'), parts along dimension 0, may hold values from -6 to 6
- out_gate: bfloat16 [4, 16, 128, 1024], P('groups', 'head', 'dim', 'seq'), parts along dimension 0, may hold values from -6 to 6
- beta: float32 [4, 16, 1024], P('groups', 'head', 'seq'), parts along dimension 0, may hold values from 0.1 to 0.9
- log_decay: float32 [4, 16, 1024], P('groups', 'head', 'seq'), parts along dimension 0, may hold values from -1 to 0, as said below
- lengths: int32 [4, 4], P('groups', 'seq'), parts along dimension 0, may hold values from 128 to 256
- norm_gain: float32 [128], P('dim'), may hold values from 0.1 to 1.9
Outputs:
- output: bfloat16 [4, 16, 128, 1024], P('groups', 'head', 'dim', 'seq'), parts along dimension 0
There are 2 independent parts, one for each index of `groups`. A program takes and returns all parts, laid end to end along the dimension named above; an argument that names none is the same for every part. Nothing has to cross between parts.
Inputs may be any that keep to these rules, and one draw needn't show every extreme that they name: `log_decay`: negative.
All inputs are finite; a program needn't handle non-finite values.
Results may differ from a plain program's by a relative error of at most 0.001.
Values sent between devices are 32-bit elements; how exact they have to be, the bound alone decides.
A program may use at most 64 MiB of HBM per device.

v0:
```python
import functools

import jax
import jax.numpy as jnp
from jax import lax
from jax.experimental import pallas as pl
from jax.experimental.pallas import tpu as pltpu
from jax.sharding import PartitionSpec as P

WINDOW = 4
GROUP = 4
HOP_LAG = 1
EPS = 1e-06
F32 = jnp.float32
BF16 = jnp.bfloat16


def dot(left, right):
    return jnp.dot(left, right, preferred_element_type=F32)


def dot_nt(left, right):
    return lax.dot_general(left, right, (((1,), (1,)), ((), ())), preferred_element_type=F32)


def split(x):
    high = x.astype(BF16)
    return high, (x - high.astype(F32)).astype(BF16)


def expand(x):
    half = x.shape[0]
    zero = jnp.zeros((half, half), x.dtype)
    return jnp.concatenate(
        [
            jnp.concatenate([x[:, :half], zero], axis=1),
            jnp.concatenate([zero, x[:, half:]], axis=1),
        ],
        axis=0,
    )


def level_masks(half):
    row = lax.broadcasted_iota(jnp.int32, (half, 2 * half), 0)
    col = lax.broadcasted_iota(jnp.int32, (half, 2 * half), 1)
    col = jnp.where(col >= half, col - half, col)
    differ = jnp.bitwise_xor(row, col)
    masks = [differ == 0]
    size = 1
    while size < half:
        masks.append((differ >= size) & (differ < 2 * size))
        size *= 2
    return [jnp.where(m, 1.0, 0.0).astype(BF16) for m in masks]


def tri_masks(half):
    row = lax.broadcasted_iota(jnp.int32, (half, half), 0)
    col = lax.broadcasted_iota(jnp.int32, (half, half), 1)
    return [jnp.where(m, 1.0, 0.0) for m in (row < col, row <= col, row == col)]


def local_terms(items, masks, tri):
    strict, incl, eye = tri
    tokens = items[0][1].shape[0]
    half = tokens // 2
    stage = []
    for q, k, v, rate, cum in items:
        kf = k.astype(F32)
        kt = kf.T
        r_row = lax.rsqrt(jnp.sum(kt * kt, axis=0, keepdims=True) + EPS)
        r_col = lax.rsqrt(jnp.sum(kf * kf, axis=1, keepdims=True) + EPS)
        cum1, cum2 = cum[:, :half], cum[:, half:]
        col1 = jnp.sum(eye * cum1, axis=1, keepdims=True)
        col2 = jnp.sum(eye * cum2, axis=1, keepdims=True)
        d11 = jnp.exp(jnp.minimum(cum1 - col1, 0.0)) * r_col[:half]
        d12 = jnp.exp(jnp.minimum(cum2 - col1, 0.0)) * r_col[:half]
        d22 = jnp.exp(jnp.minimum(cum2 - col2, 0.0)) * r_col[half:]
        k1, k2 = k[:half], k[half:]
        gk1, gq1 = dot_nt(k1, k), dot_nt(k1, q)
        gk2, gq2 = dot_nt(k2, k2), dot_nt(k2, q[half:])
        rr = rate * r_row
        l11 = strict * (d11 * gk1[:, :half]) * rr[:, :half]
        l12 = d12 * gk1[:, half:] * rr[:, half:]
        l22 = strict * (d22 * gk2) * rr[:, half:]
        p11 = incl * (d11 * gq1[:, :half])
        p12 = d12 * gq1[:, half:]
        p22 = incl * (d22 * gq2)
        zero = jnp.zeros((half, half), BF16)

        def whole(a, b, c):
            top = split(jnp.concatenate([a, b], axis=1))
            low = split(c)
            return [
                jnp.concatenate([t, jnp.concatenate([zero, u], axis=1)], axis=0)
                for t, u in zip(top, low)
            ]

        l_hi, l_lo = whole(l11, l12, l22)
        p_hi, p_lo = whole(p11, p12, p22)
        lc = jnp.concatenate([l_hi[:half, :half], l_hi[half:, half:]], axis=1)
        rhs = jnp.concatenate([v.astype(F32) * rate, kt * (rr * jnp.exp(cum))], axis=0)
        tail = jnp.exp(cum[:, tokens - 1 :] - cum) * r_row
        stage.append((k, l_hi, l_lo, p_hi, p_lo, lc, rhs, tail))
    inv = [masks[0] - s[5] * masks[1] for s in stage]
    for mask in masks[2:]:
        mid = [dot(s[5] * mask, expand(x)).astype(BF16) for s, x in zip(stage, inv)]
        inv = [x - dot(x, expand(z)).astype(BF16) for x, z in zip(inv, mid)]
    corner = [dot(x[:, :half], s[1][:half, half:]).astype(BF16) for s, x in zip(stage, inv)]
    corner = [(-dot(c, x[:, half:])).astype(BF16) for c, x in zip(corner, inv)]
    full = []
    for x, c in zip(inv, corner):
        zero = jnp.zeros((half, half), BF16)
        full.append(
            jnp.concatenate(
                [
                    jnp.concatenate([x[:, :half], c], axis=1),
                    jnp.concatenate([zero, x[:, half:]], axis=1),
                ],
                axis=0,
            )
        )
    first = [dot(s[6].astype(BF16), x).astype(BF16) for s, x in zip(stage, full)]
    rest = [
        s[6] - y.astype(F32) - (dot(y, s[1]) + dot(y, s[2])) for s, y in zip(stage, first)
    ]
    solved = [y.astype(F32) + dot(r.astype(BF16), x) for y, r, x in zip(first, rest, full)]
    results = []
    for (k, _, _, p_hi, p_lo, _, rhs, tail), y in zip(stage, solved):
        rows = y.shape[0]
        t_hi, t_lo = split(y * tail)
        on_key = dot(jnp.concatenate([t_hi, t_lo], axis=0), k)
        y_hi, y_lo = split(y)
        on_query = dot(jnp.concatenate([y_hi, y_lo], axis=0), p_hi)
        results.append(
            (
                on_key[:rows] + on_key[rows:],
                on_query[:rows] + on_query[rows:] + dot(y_hi, p_lo),
            )
        )
    return results


def times(left, right_hi, right_lo):
    rows = left.shape[0]
    hi, lo = split(left)
    both = dot(jnp.concatenate([hi, lo], axis=0), right_hi)
    return both[:rows] + both[rows:] + dot(hi, right_lo)


def body(
    n_seq, hops, per_seq, val_total,
    value, beta, decay, query_hbm, key_hbm, lengths, out,
    query, key, mask_buf, tri_buf, rate_buf, cum_buf, live_buf,
    end_buf, map_hi, map_lo, raw_buf, read_hi, read_lo,
    arrive, depart, val_send, val_recv, out_send, out_recv,
    load_sem, send_sem, recv_sem, val_send_sem, val_recv_sem, out_send_sem, out_recv_sem,
):
    own, tokens, key_width = key.shape
    val_width = value.shape[1]
    half = tokens // 2
    me = lax.axis_index("seq")
    core = lax.axis_index("dim")
    peer = 1 - core
    base, peer_base = core * own, peer * own
    has_left, has_right = me > 0, me < n_seq - 1

    def load(source, target, index):
        return pltpu.make_async_copy(source.at[pl.ds(base, own)], target, load_sem.at[index])

    load(key_hbm, key, 0).start()
    load(query_hbm, query, 1).start()

    barrier = pltpu.get_barrier_semaphore()

    @pl.when(has_right)
    def _():
        pl.semaphore_signal(barrier, inc=1, device_id={"seq": me + 1})

    @pl.when(has_left)
    def _():
        pl.semaphore_signal(barrier, inc=1, device_id={"seq": me - 1})

    pl.semaphore_signal(barrier, inc=1, device_id={"dim": peer})

    for p in range(own):
        val_send[p] = value[peer_base + p].astype(F32)
    for index, mask in enumerate(level_masks(half)):
        mask_buf[index] = mask
    for index, mask in enumerate(tri_masks(half)):
        tri_buf[index] = mask
    position = lax.broadcasted_iota(jnp.int32, (per_seq, tokens), 1)
    for b in range(2 * own // per_seq):
        live = jnp.where(position < lengths[0, b], 1.0, 0.0)
        rows = pl.ds(b * per_seq, per_seq)
        live_buf[rows, :] = live
        rate_buf[rows, :] = beta[rows, :] * live
        cum_buf[rows, :] = decay[rows, :] * live
    row = lax.broadcasted_iota(jnp.int32, (tokens, tokens), 0)
    col = lax.broadcasted_iota(jnp.int32, (tokens, tokens), 1)
    upto = jnp.where(row <= col, 1.0, 0.0)
    cum_buf[...] = jnp.dot(
        cum_buf[...], upto, precision=lax.Precision.HIGHEST, preferred_element_type=F32
    )

    pl.semaphore_wait(barrier, 1 + has_left.astype(jnp.int32) + has_right.astype(jnp.int32))

    def remote(source, target, sent, received, p, where):
        return pltpu.make_async_remote_copy(
            src_ref=source.at[p],
            dst_ref=target.at[p],
            send_sem=sent.at[p],
            recv_sem=received.at[p],
            device_id=where,
        )

    def state_copy(p):
        return remote(depart, arrive, send_sem, recv_sem, p, {"seq": me + 1})

    def value_copy(p):
        return remote(val_send, val_recv, val_send_sem, val_recv_sem, p, {"dim": peer})

    def out_copy(p):
        return remote(out_send, out_recv, out_send_sem, out_recv_sem, p, {"dim": peer})

    for p in range(own):
        value_copy(p).start()

    @pl.when(jnp.logical_not(has_left))
    def _():
        arrive[...] = jnp.zeros_like(arrive)

    load(key_hbm, key, 0).wait()
    load(query_hbm, query, 1).wait()

    def row_of(ref, p):
        return ref[pl.ds(base + p, 1), :]

    def compute(g):
        ids = [g * GROUP + u for u in range(GROUP)]
        for p in ids:
            value_copy(p).wait_recv()
        items = []
        for p in ids:
            val = jnp.concatenate([value[base + p].astype(F32), val_recv[p]], axis=0)
            items.append((query[p], key[p], val, row_of(rate_buf, p), row_of(cum_buf, p)))
        masks = [mask_buf[index] for index in range(mask_buf.shape[0])]
        results = local_terms(items, masks, [tri_buf[index] for index in range(3)])
        for p, (on_key, on_query) in zip(ids, results):
            end_buf[p] = on_key[:val_total]
            map_hi[p], map_lo[p] = split(on_key[val_total:])
            raw_buf[p] = on_query[:val_total]
            read_hi[p], read_lo[p] = split(on_query[val_total:])

    def pass_on(p):
        @pl.when(has_left)
        def _():
            state_copy(p).wait_recv()

        came = [arrive[p, h] for h in range(hops)]
        start = functools.reduce(jnp.add, came)
        cum = row_of(cum_buf, p)
        decayed = jnp.exp(cum[:, tokens - 1 :])
        if hops == 1:
            moved = decayed * start - times(start, map_hi[p], map_lo[p])
            depart[p, 0] = end_buf[p] + moved
        else:
            depart[p, 0] = end_buf[p]
            moving = jnp.concatenate(came[: hops - 1], axis=0)
            moved = decayed * moving - times(moving, map_hi[p], map_lo[p])
            for h in range(hops - 1):
                depart[p, h + 1] = moved[h * val_total : (h + 1) * val_total]

        @pl.when(has_right)
        def _():
            state_copy(p).start()

        hi, lo = split(start)
        direct = dot_nt(jnp.concatenate([hi, lo], axis=0), query[p])
        direct = (direct[:val_total] + direct[val_total:]) * jnp.exp(cum)
        raw = raw_buf[p] + direct - times(start, read_hi[p], read_lo[p])
        total = jnp.sum(raw * raw, axis=0, keepdims=True)
        normed = raw * (lax.rsqrt(total / val_total + EPS) * row_of(live_buf, p))
        out[base + p] = normed[:val_width]
        out_send[p] = normed[val_width:]
        out_copy(p).start()

    groups = own // GROUP
    lag = me * HOP_LAG

    def step(i, carry):
        @pl.when(i < groups)
        def _():
            compute(i)

        @pl.when(i >= lag)
        def _():
            for u in range(GROUP):
                pass_on((i - lag) * GROUP + u)

        return carry

    lax.fori_loop(0, groups + lag, step, 0)

    for p in range(own):
        out_copy(p).wait_recv()
        out[peer_base + p] = out_recv[p]

    def drain(p, carry):
        @pl.when(has_right)
        def _():
            state_copy(p).wait_send()

        value_copy(p).wait_send()
        out_copy(p).wait_send()
        return carry

    lax.fori_loop(0, own, drain, 0)


def solution(mesh):
    n_seq, n_dim = mesh.shape["seq"], mesh.shape["dim"]
    hops = 1 if n_seq <= WINDOW + 1 else WINDOW

    def local(query, key, value, out_gate, beta, log_decay, lengths, norm_gain):
        seqs, heads, tokens, key_width = query.shape
        val_width = value.shape[2]
        val_total = val_width * n_dim
        pairs = seqs * heads
        own = pairs // n_dim
        half = tokens // 2
        vmem = pl.BlockSpec(memory_space=pltpu.VMEM)
        anywhere = pl.BlockSpec(memory_space=pl.ANY)
        flat = lambda x: x.reshape((pairs,) + x.shape[2:])
        dma = pltpu.SemaphoreType.DMA
        normed = pl.pallas_call(
            functools.partial(body, n_seq, hops, heads, val_total),
            out_shape=jax.ShapeDtypeStruct((pairs, val_width, tokens), F32),
            in_specs=[vmem] * 3 + [anywhere] * 2 + [pl.BlockSpec(memory_space=pltpu.SMEM)],
            out_specs=vmem,
            scratch_shapes=[
                pltpu.VMEM((own, tokens, key_width), BF16),
                pltpu.VMEM((own, tokens, key_width), BF16),
                pltpu.VMEM((half.bit_length(), half, tokens), BF16),
                pltpu.VMEM((3, half, half), F32),
                pltpu.VMEM((pairs, tokens), F32),
                pltpu.VMEM((pairs, tokens), F32),
                pltpu.VMEM((pairs, tokens), F32),
                pltpu.VMEM((own, val_total, key_width), F32),
                pltpu.VMEM((own, key_width, key_width), BF16),
                pltpu.VMEM((own, key_width, key_width), BF16),
                pltpu.VMEM((own, val_total, tokens), F32),
                pltpu.VMEM((own, key_width, tokens), BF16),
                pltpu.VMEM((own, key_width, tokens), BF16),
                pltpu.VMEM((own, hops, val_total, key_width), F32),
                pltpu.VMEM((own, hops, val_total, key_width), F32),
                pltpu.VMEM((own, val_width, tokens), F32),
                pltpu.VMEM((own, val_width, tokens), F32),
                pltpu.VMEM((own, val_width, tokens), F32),
                pltpu.VMEM((own, val_width, tokens), F32),
                dma((2,)),
                dma((own,)),
                dma((own,)),
                dma((own,)),
                dma((own,)),
                dma((own,)),
                dma((own,)),
            ],
            compiler_params=pltpu.CompilerParams(
                collective_id=0, has_side_effects=True, vmem_limit_bytes=60 * 1024 * 1024
            ),
        )(flat(value), flat(beta), flat(log_decay), flat(query), flat(key), lengths.T)
        normed = normed.reshape(value.shape)
        gated = normed * norm_gain[None, None, :, None] * jax.nn.silu(out_gate.astype(F32))
        return gated.astype(BF16)

    in_specs = (
        P("groups", "head", "seq", None),
        P("groups", "head", "seq", None),
        P("groups", "head", "dim", "seq"),
        P("groups", "head", "dim", "seq"),
        P("groups", "head", "seq"),
        P("groups", "head", "seq"),
        P("groups", "seq"),
        P("dim"),
    )
    out_specs = P("groups", "head", "dim", "seq")
    return jax.shard_map(local, mesh=mesh, in_specs=in_specs, out_specs=out_specs, check_vma=False)
```

profile of v0, /device:TPU:31, one launch (start us, length us, event | category | flops | bytes accessed | tf_op | source)
XLA Modules:
  0.0 35.3 jit_solution(6908899185820528335)
XLA Ops:
  0.0 0.0 copy-start
  0.0 32.2 %shard_map.82 = f32[16,64,256]{2,1,0:T(8,128)} custom-call(bf16[16,64,256]{2,1,0:T(8,128)(2,1)} %bitcast.10, f32[16,256]{1,0:T(8,128)} %bitcast.11, f32[16,256]{1,0:T(8,128)} %bitcast.12, bf16[16,256,128]{2,1,0:T(8,128)(2,1)} %bitcast.8, bf16[16,256,128]{2,1,0:T(8,128)(2,1)} %bitcast.9, s32[1,2]{1,0:T(1,128)} %bitcast.13), custom_call_target="tpu_custom_call" | custom-call | tf_op jit(solution)/shard_map/pallas_call | solution.py:335
  32.2 0.0 copy-start.1
  32.2 0.0 copy-done
  32.2 0.6 %copy-done.1 = f32[64]{0:T(128)S(1)} copy-done((f32[64]{0:T(128)S(1)}, f32[64]{0:T(128)}, u32[]{:S(2)}) %copy-start.1) | copy-done | bytes 280
  32.9 2.4 %fusion.4 = bf16[2,8,64,256]{3,2,1,0:T(8,128)(2,1)} fusion(bf16[2,8,64,256]{3,2,1,0:T(8,128)(2,1)S(1)} %copy-done, f32[2,8,64,256]{3,2,1,0:T(8,128)} %bitcast.7, f32[64]{0:T(128)S(1)} %copy-done.1), kind=kLoop, calls=%fused_computation.6 | loop fusion | flops 2097152 | bytes 2097408 | tf_op jit(solution)/shard_map/convert_element_type | solution.py:374
Async XLA Ops:
  0.0 32.2 %copy-start = (bf16[2,8,64,256]{3,2,1,0:T(8,128)(2,1)S(1)}, bf16[2,8,64,256]{3,2,1,0:T(8,128)(2,1)}, u32[]{:S(2)}) copy-start(bf16[2,8,64,256]{3,2,1,0:T(8,128)(2,1)} %param.11) | copy-start | bytes 1572868
  32.2 0.7 %copy-start.1 = (f32[64]{0:T(128)S(1)}, f32[64]{0:T(128)}, u32[]{:S(2)}) copy-start(f32[64]{0:T(128)} %param.15) | copy-start | bytes 772
where the time goes:
time: 35.4 us; the launch traced here: 35.3 us
  Pallas kernels  32.2 us (91%)
  other arithmetic  2.41 us (7%)
  local copies, waits for them, and re-layouts  0.64 us (2%)
    pallas_call x1, Pallas kernels, local(): pl.pallas_call(functools.partial(body, n_seq, hops, heads, val_total), ou...  32.2 us
    convert_element_type x1, other arithmetic, local(): return gated.astype(BF16)  2.41 us

commit v1 on v0

v1 whole, which is shorter than its diff:
```python
import functools

import jax
import jax.numpy as jnp
from jax import lax
from jax.experimental import pallas as pl
from jax.experimental.pallas import tpu as pltpu
from jax.sharding import PartitionSpec as P

WINDOW = 4
GROUP = 4
BASE = 16
TILE = 8
EPS = 1e-06
F32 = jnp.float32
BF16 = jnp.bfloat16


def dot(left, right):
    return jnp.dot(left, right, preferred_element_type=F32)


def dot_nt(left, right):
    return lax.dot_general(left, right, (((1,), (1,)), ((), ())), preferred_element_type=F32)


def split(x):
    high = x.astype(BF16)
    return high, (x - high.astype(F32)).astype(BF16)


def expand(x):
    half = x.shape[0]
    zero = jnp.zeros((half, half), x.dtype)
    return jnp.concatenate(
        [
            jnp.concatenate([x[:, :half], zero], axis=1),
            jnp.concatenate([zero, x[:, half:]], axis=1),
        ],
        axis=0,
    )


def corner_block(a, b, c):
    zero = jnp.zeros((c.shape[0], a.shape[1]), c.dtype)
    return jnp.concatenate(
        [jnp.concatenate([a, b], axis=1), jnp.concatenate([zero, c], axis=1)], axis=0
    )


def level_masks(half):
    row = lax.broadcasted_iota(jnp.int32, (half, 2 * half), 0)
    col = lax.broadcasted_iota(jnp.int32, (half, 2 * half), 1)
    col = jnp.where(col >= half, col - half, col)
    differ = jnp.bitwise_xor(row, col)
    masks = []
    size = BASE
    while size < half:
        masks.append((differ >= size) & (differ < 2 * size))
        size *= 2
    return [jnp.where(m, 1.0, 0.0).astype(BF16) for m in masks]


def tri_masks(half):
    row = lax.broadcasted_iota(jnp.int32, (half, half), 0)
    col = lax.broadcasted_iota(jnp.int32, (half, half), 1)
    return [jnp.where(m, 1.0, 0.0) for m in (row < col, row <= col, row == col)]


def block_ones(tokens):
    row = lax.broadcasted_iota(jnp.int32, (tokens, tokens), 0)
    col = lax.broadcasted_iota(jnp.int32, (tokens, tokens), 1)
    return jnp.where(jnp.bitwise_xor(row, col) < BASE, 1.0, 0.0).astype(BF16)


def lane_of(rows, tokens):
    return lax.broadcasted_iota(jnp.int32, (rows, tokens), 1)


def base_rows(packed):
    half, tokens = packed.shape
    lane = lane_of(BASE, tokens)
    block = jnp.bitwise_and(lane, half - 1) // BASE
    compact = jnp.zeros((BASE, tokens), F32)
    for b in range(half // BASE):
        compact = jnp.where(block == b, packed[b * BASE : (b + 1) * BASE], compact)
    inner = jnp.bitwise_and(lane, BASE - 1)
    pieces = []
    for j in range(1, BASE):
        rows = TILE if j <= TILE else BASE
        pieces.append(jnp.where(inner[:rows] == j, compact[:rows], 0.0))
    return jnp.concatenate(pieces, axis=0).astype(BF16)


def base_inverse(spread, half):
    tokens = spread.shape[1]
    offset, place = {}, 0
    for j in range(1, BASE):
        offset[j] = place
        place += TILE if j <= TILE else BASE
    lane = jnp.bitwise_and(lane_of(TILE, tokens), BASE - 1)
    row = lax.broadcasted_iota(jnp.int32, (TILE, tokens), 0)
    top = jnp.where(lane == row, 1.0, 0.0)
    low = jnp.where(lane == row + TILE, 1.0, 0.0)
    for j in range(BASE - 1, 0, -1):
        at = offset[j]
        if j > TILE:
            line = low[j - TILE : j - TILE + 1]
            low = low - spread[at + TILE : at + BASE] * line
        else:
            line = low[:1] if j == TILE else top[j : j + 1]
        top = top - spread[at : at + TILE] * line
    found = jnp.concatenate([top, low], axis=0)
    lane = lane_of(BASE, tokens)
    block = jnp.bitwise_and(lane, half - 1) // BASE
    return jnp.concatenate(
        [jnp.where(block == b, found, 0.0) for b in range(half // BASE)], axis=0
    ).astype(BF16)


def key_terms(items, masks, ones, tri):
    strict, _, eye = tri
    tokens = items[0][0].shape[0]
    half = tokens // 2
    stage = []
    for k, rate, cum in items:
        cum1, cum2 = cum[:, :half], cum[:, half:]
        col1 = jnp.sum(eye * cum1, axis=1, keepdims=True)
        col2 = jnp.sum(eye * cum2, axis=1, keepdims=True)
        d11 = jnp.exp(jnp.minimum(cum1 - col1, 0.0))
        d12 = jnp.exp(jnp.minimum(cum2 - col1, 0.0))
        d22 = jnp.exp(jnp.minimum(cum2 - col2, 0.0))
        top = dot_nt(k[:half], k)
        g22 = dot_nt(k[half:], k[half:])
        norm = jnp.concatenate(
            [
                jnp.sum(eye * top[:, :half], axis=0, keepdims=True),
                jnp.sum(eye * g22, axis=0, keepdims=True),
            ],
            axis=1,
        )
        r = lax.rsqrt(norm + EPS)
        w = rate * (r * r)
        l11 = strict * (d11 * top[:, :half]) * w[:, :half]
        l12 = d12 * top[:, half:] * w[:, half:]
        l22 = strict * (d22 * g22) * w[:, half:]
        packed = jnp.concatenate([l11, l22], axis=1)
        pair = [split(x) for x in (l11, l12, l22)]
        l_hi = [x[0] for x in pair]
        l_lo = [x[1] for x in pair]
        stage.append((l_hi, l_lo, packed, r, w, (d11, d12, d22)))
    spread = [dot(base_rows(s[2]), ones) for s in stage]
    inv = [base_inverse(x, half) for x in spread]
    lc = [jnp.concatenate([s[0][0], s[0][2]], axis=1) for s in stage]
    for mask in masks:
        mid = [dot(c * mask, expand(x)).astype(BF16) for c, x in zip(lc, inv)]
        inv = [x - dot(x, expand(z)).astype(BF16) for x, z in zip(inv, mid)]
    corner = [dot(x[:, :half], s[0][1]).astype(BF16) for s, x in zip(stage, inv)]
    corner = [(-dot(c, x[:, half:])).astype(BF16) for c, x in zip(corner, inv)]
    full = [corner_block(x[:, :half], c, x[:, half:]) for x, c in zip(inv, corner)]
    return stage, full


def solve_terms(stage, full, sides):
    lower = [(corner_block(*s[0]), corner_block(*s[1])) for s in stage]
    first = [dot(rhs.astype(BF16), x).astype(BF16) for rhs, x in zip(sides, full)]
    rest = [
        rhs - y.astype(F32) - (dot(y, l[0]) + dot(y, l[1]))
        for rhs, y, l in zip(sides, first, lower)
    ]
    return [y.astype(F32) + dot(r.astype(BF16), x) for y, r, x in zip(first, rest, full)]


def times(left, right_hi, right_lo):
    rows = left.shape[0]
    hi, lo = split(left)
    both = dot(jnp.concatenate([hi, lo], axis=0), right_hi)
    return both[:rows] + both[rows:] + dot(hi, right_lo)


def body(
    n_seq, hops, per_seq, val_total, group,
    value_hbm, beta_hbm, decay_hbm, gain_hbm, query_hbm, key_hbm, lengths_hbm, out,
    lengths, value, beta, decay, gain, query, key,
    mask_buf, ones_buf, tri_buf, rate_buf, cum_buf, live_buf, gain_buf,
    dec_buf, y_hi, y_lo, map_hi, map_lo, raw_buf, read_hi, read_lo,
    arrive, depart, val_send, val_recv, out_send, out_recv,
    load_sem, key_sem, send_sem, recv_sem,
    val_send_sem, val_recv_sem, out_send_sem, out_recv_sem,
):
    own, tokens, key_width = key.shape
    val_width = value.shape[1]
    half = tokens // 2
    me = lax.axis_index("seq")
    core = lax.axis_index("dim")
    peer = 1 - core
    base, peer_base = core * own, peer * own
    has_left, has_right = me > 0, me < n_seq - 1

    def load(source, target, index):
        return pltpu.make_async_copy(source, target, load_sem.at[index])

    def key_load(g):
        return pltpu.make_async_copy(
            key_hbm.at[pl.ds(base + g * group, group)],
            key.at[pl.ds(g * group, group)],
            key_sem.at[g],
        )

    mine, theirs = pl.ds(base, own), pl.ds(peer_base, own)
    loads = [
        load(value_hbm.at[theirs], value.at[theirs], 0),
        load(decay_hbm, decay, 1),
        load(beta_hbm, beta, 2),
        load(value_hbm.at[mine], value.at[mine], 3),
        load(gain_hbm, gain, 4),
        load(query_hbm.at[mine], query, 5),
        load(lengths_hbm, lengths, 6),
    ]
    for copy in loads[:3] + loads[6:]:
        copy.start()
    for g in range(own // group):
        key_load(g).start()
    for copy in loads[3:6]:
        copy.start()

    barrier = pltpu.get_barrier_semaphore()

    @pl.when(has_right)
    def _():
        pl.semaphore_signal(barrier, inc=1, device_id={"seq": me + 1})

    @pl.when(has_left)
    def _():
        pl.semaphore_signal(barrier, inc=1, device_id={"seq": me - 1})

    pl.semaphore_signal(barrier, inc=1, device_id={"dim": peer})

    for index, mask in enumerate(level_masks(half)):
        mask_buf[index] = mask
    for index, mask in enumerate(tri_masks(half)):
        tri_buf[index] = mask
    ones_buf[...] = block_ones(tokens)

    if hops > 1:

        @pl.when(jnp.logical_not(has_left))
        def _():
            depart[...] = jnp.zeros_like(depart)

    loads[0].wait()
    for p in range(own):
        val_send[p] = value[peer_base + p].astype(F32)
    loads[1].wait()
    loads[2].wait()
    loads[6].wait()
    position = lax.broadcasted_iota(jnp.int32, (per_seq, tokens), 1)
    for b in range(2 * own // per_seq):
        live = jnp.where(position < lengths[0, b], 1.0, 0.0)
        rows = pl.ds(b * per_seq, per_seq)
        live_buf[rows, :] = live
        rate_buf[rows, :] = beta[rows, :] * live
        cum_buf[rows, :] = decay[rows, :] * live

    pl.semaphore_wait(barrier, 1 + has_left.astype(jnp.int32) + has_right.astype(jnp.int32))

    def remote(source, target, sent, received, p, where):
        return pltpu.make_async_remote_copy(
            src_ref=source.at[p],
            dst_ref=target.at[p],
            send_sem=sent.at[p],
            recv_sem=received.at[p],
            device_id=where,
        )

    def state_copy(p):
        return remote(depart, arrive, send_sem, recv_sem, p, {"seq": me + 1})

    def value_copy(p):
        return remote(val_send, val_recv, val_send_sem, val_recv_sem, p, {"dim": peer})

    def out_copy(p):
        return remote(out_send, out_recv, out_send_sem, out_recv_sem, p, {"dim": peer})

    for p in range(own):
        value_copy(p).start()

    row = lax.broadcasted_iota(jnp.int32, (tokens, tokens), 0)
    col = lax.broadcasted_iota(jnp.int32, (tokens, tokens), 1)
    upto = jnp.where(row <= col, 1.0, 0.0)
    cum_buf[...] = jnp.dot(
        cum_buf[...], upto, precision=lax.Precision.HIGHEST, preferred_element_type=F32
    )
    loads[4].wait()
    row = lax.broadcasted_iota(jnp.int32, (val_width, val_width), 0)
    col = lax.broadcasted_iota(jnp.int32, (val_width, val_width), 1)
    gain_col = jnp.sum(jnp.where(row == col, gain[...], 0.0), axis=1, keepdims=True)
    gain_buf[...] = jnp.broadcast_to(gain_col, gain_buf.shape)
    loads[3].wait()

    def row_of(ref, p):
        return ref[pl.ds(base + p, 1), :]

    def key_phase(g, carry):
        ids = [g * group + u for u in range(group)]
        key_load(g).wait()
        items = [(key[p], row_of(rate_buf, p), row_of(cum_buf, p)) for p in ids]
        masks = [mask_buf[index] for index in range(mask_buf.shape[0])]
        tri = [tri_buf[index] for index in range(3)]
        stage, full = key_terms(items, masks, ones_buf[...], tri)
        for p, s in zip(ids, stage):
            for index, block in enumerate(s[5]):
                dec_buf[p, index] = block
        for p in ids:
            value_copy(p).wait_recv()
        sides = []
        for p, s, (k, rate, cum) in zip(ids, stage, items):
            val = jnp.concatenate([value[base + p].astype(F32), val_recv[p]], axis=0)
            kt = k.astype(F32).T
            sides.append(
                jnp.concatenate([val * (rate * s[3]), kt * (s[4] * jnp.exp(cum))], axis=0)
            )
        solved = solve_terms(stage, full, sides)
        for p, y, (k, rate, cum) in zip(ids, solved, items):
            tail = jnp.exp(cum[:, tokens - 1 :] - cum)
            t_hi, t_lo = split(y * tail)
            rows = y.shape[0]
            on_key = dot(jnp.concatenate([t_hi, t_lo], axis=0), k)
            on_key = on_key[:rows] + on_key[rows:]
            depart[p, 0] = on_key[:val_total]
            map_hi[p], map_lo[p] = split(on_key[val_total:])
            y_hi[p], y_lo[p] = split(y)

        @pl.when(jnp.logical_and(jnp.logical_not(has_left), has_right))
        def _():
            for p in ids:
                state_copy(p).start()

        return carry

    lax.fori_loop(0, own // group, key_phase, 0)
    loads[5].wait()

    def query_phase(p):
        q, k, cum = query[p], key[p], row_of(cum_buf, p)
        top = dot_nt(k[:half], q)
        g22 = dot_nt(k[half:], q[half:])
        incl = tri_buf[1]
        p11 = split(incl * (dec_buf[p, 0] * top[:, :half]))
        p12 = split(dec_buf[p, 1] * top[:, half:])
        p22 = split(incl * (dec_buf[p, 2] * g22))
        p_hi = corner_block(p11[0], p12[0], p22[0])
        p_lo = corner_block(p11[1], p12[1], p22[1])
        hi, lo = y_hi[p], y_lo[p]
        rows = hi.shape[0]
        both = dot(jnp.concatenate([hi, lo], axis=0), p_hi)
        on_query = both[:rows] + both[rows:] + dot(hi, p_lo)
        raw_buf[p] = on_query[:val_total]
        read = q.astype(F32).T * jnp.exp(cum) - on_query[val_total:]
        read_hi[p], read_lo[p] = split(read)

    def pass_on(p):
        state_copy(p).wait_recv()

        @pl.when(has_right)
        def _():
            cum = row_of(cum_buf, p)
            decayed = jnp.exp(cum[:, tokens - 1 :])
            if hops == 1:
                start = arrive[p, 0]
                moved = decayed * start - times(start, map_hi[p], map_lo[p])
                depart[p, 0] = depart[p, 0] + moved
            else:
                moving = jnp.concatenate([arrive[p, h] for h in range(hops - 1)], axis=0)
                moved = decayed * moving - times(moving, map_hi[p], map_lo[p])
                for h in range(hops - 1):
                    depart[p, h + 1] = moved[h * val_total : (h + 1) * val_total]
            state_copy(p).start()

        start = functools.reduce(jnp.add, [arrive[p, h] for h in range(hops)])
        raw_buf[p] = raw_buf[p] + times(start, read_hi[p], read_lo[p])

    def finish(p):
        raw = raw_buf[p]
        total = jnp.sum(raw * raw, axis=0, keepdims=True)
        normed = raw * (lax.rsqrt(total / val_total + EPS) * row_of(live_buf, p))
        out[base + p] = normed[:val_width] * gain_buf[...]
        out_send[p] = normed[val_width:]
        out_copy(p).start()

    def step(p, carry):
        query_phase(p)

        @pl.when(has_left)
        def _():
            pass_on(p)

        finish(p)
        return carry

    lax.fori_loop(0, own, step, 0)

    def drain(p, carry):
        @pl.when(has_right)
        def _():
            state_copy(p).wait_send()

        value_copy(p).wait_send()
        out_copy(p).wait_send()
        out_copy(p).wait_recv()
        out[peer_base + p] = out_recv[p] * gain_buf[...]
        return carry

    lax.fori_loop(0, own, drain, 0)


def solution(mesh):
    n_seq, n_dim = mesh.shape["seq"], mesh.shape["dim"]
    hops = 1 if n_seq <= WINDOW + 1 else WINDOW

    def local(query, key, value, out_gate, beta, log_decay, lengths, norm_gain):
        seqs, heads, tokens, key_width = query.shape
        val_width = value.shape[2]
        val_total = val_width * n_dim
        pairs = seqs * heads
        own = pairs // n_dim
        half = tokens // 2
        group = max(g for g in range(1, GROUP + 1) if own % g == 0)
        levels = (half // BASE).bit_length() - 1
        vmem = pl.BlockSpec(memory_space=pltpu.VMEM)
        anywhere = pl.BlockSpec(memory_space=pl.ANY)
        dma = pltpu.SemaphoreType.DMA
        flat = lambda x: x.reshape((pairs,) + x.shape[2:])
        hold = lambda x: pltpu.with_memory_space_constraint(x, pltpu.HBM)
        operands = [flat(value), flat(beta), flat(log_decay), norm_gain[None, :]]
        operands += [flat(query), flat(key), lengths.T]
        normed = pl.pallas_call(
            functools.partial(body, n_seq, hops, heads, val_total, group),
            out_shape=pltpu.VMEM((pairs, val_width, tokens), F32),
            in_specs=[anywhere] * 7,
            out_specs=vmem,
            scratch_shapes=[
                pltpu.SMEM((1, seqs), jnp.int32),
                pltpu.VMEM((pairs, val_width, tokens), BF16),
                pltpu.VMEM((pairs, tokens), F32),
                pltpu.VMEM((pairs, tokens), F32),
                pltpu.VMEM((1, val_width), F32),
                pltpu.VMEM((own, tokens, key_width), BF16),
                pltpu.VMEM((own, tokens, key_width), BF16),
                pltpu.VMEM((levels, half, tokens), BF16),
                pltpu.VMEM((tokens, tokens), BF16),
                pltpu.VMEM((3, half, half), F32),
                pltpu.VMEM((pairs, tokens), F32),
                pltpu.VMEM((pairs, tokens), F32),
                pltpu.VMEM((pairs, tokens), F32),
                pltpu.VMEM((val_width, tokens), F32),
                pltpu.VMEM((own, 3, half, half), F32),
                pltpu.VMEM((own, val_total + key_width, tokens), BF16),
                pltpu.VMEM((own, val_total + key_width, tokens), BF16),
                pltpu.VMEM((own, key_width, key_width), BF16),
                pltpu.VMEM((own, key_width, key_width), BF16),
                pltpu.VMEM((own, val_total, tokens), F32),
                pltpu.VMEM((own, key_width, tokens), BF16),
                pltpu.VMEM((own, key_width, tokens), BF16),
                pltpu.VMEM((own, hops, val_total, key_width), F32),
                pltpu.VMEM((own, hops, val_total, key_width), F32),
                pltpu.VMEM((own, val_width, tokens), F32),
                pltpu.VMEM((own, val_width, tokens), F32),
                pltpu.VMEM((own, val_width, tokens), F32),
                pltpu.VMEM((own, val_width, tokens), F32),
                dma((7,)),
                dma((own // group,)),
                dma((own,)),
                dma((own,)),
                dma((own,)),
                dma((own,)),
                dma((own,)),
                dma((own,)),
            ],
            compiler_params=pltpu.CompilerParams(
                collective_id=0, has_side_effects=True, vmem_limit_bytes=48 * 1024 * 1024
            ),
        )(*[hold(x) for x in operands])
        normed = normed.reshape(value.shape)
        gated = normed * jax.nn.silu(out_gate.astype(F32))
        return gated.astype(BF16)

    in_specs = (
        P("groups", "head", "seq", None),
        P("groups", "head", "seq", None),
        P("groups", "head", "dim", "seq"),
        P("groups", "head", "dim", "seq"),
        P("groups", "head", "seq"),
        P("groups", "head", "seq"),
        P("groups", "seq"),
        P("dim"),
    )
    out_specs = P("groups", "head", "dim", "seq")
    return jax.shard_map(local, mesh=mesh, in_specs=in_specs, out_specs=out_specs, check_vma=False)
```

time: 35.4 us -> 27.8 us (0.79)
  Pallas kernels: 32.2 us -> 26.5 us
  other arithmetic: 2.41 us -> 1.13 us
  local copies, waits for them, and re-layouts: 0.64 us -> 0.01 us
    pallas_call x1, Pallas kernels: 32.2 us -> 26.5 us  [local(): pl.pallas_call(functools.partial(body, n_seq, hops, heads, val_total, gro...]
    convert_element_type x1, other arithmetic: 2.41 us -> 1.13 us  [local(): return gated.astype(BF16)]
    unnamed x4 -> x2, local copies, waits for them, and re-layouts: 0.64 us -> 0.01 us
where the time goes in v1:
time: 27.8 us; the launch traced here: 27.6 us
  Pallas kernels  26.5 us (95%)
  other arithmetic  1.13 us (4%)
    pallas_call x1, Pallas kernels, local(): pl.pallas_call(functools.partial(body, n_seq, hops, heads, val_total, gro...  26.5 us
    convert_element_type x1, other arithmetic, local(): return gated.astype(BF16)  1.13 us

profile of v1, /device:TPU:31, one launch (start us, length us, event | category | flops | bytes accessed | tf_op | source)
XLA Modules:
  0.0 27.6 jit_solution(945460579805098607)
XLA Ops:
  0.0 0.0 copy-start
  0.0 26.5 %shard_map.82 = f32[16,64,256]{2,1,0:T(8,128)S(1)} custom-call(bf16[16,64,256]{2,1,0:T(8,128)(2,1)} %bitcast.11, f32[16,256]{1,0:T(8,128)} %bitcast.12, f32[16,256]{1,0:T(8,128)} %bitcast.13, f32[1,64]{1,0:T(1,128)} %bitcast.14, bf16[16,256,128]{2,1,0:T(8,128)(2,1)} %bitcast.9, bf16[16,256,128]{2,1,0:T(8,128)(2,1)} %bitcast.10, s32[1,2]{1,0:T(1,128)} %bitcast.15), custom_call_target="tpu_custom_call" | custom-call | tf_op jit(solution)/shard_map/pallas_call | solution.py:437
  26.5 0.0 copy-done
  26.5 1.1 %fusion.4 = bf16[2,8,64,256]{3,2,1,0:T(8,128)(2,1)} fusion(f32[2,8,64,256]{3,2,1,0:T(8,128)S(1)} %bitcast.8, bf16[2,8,64,256]{3,2,1,0:T(8,128)(2,1)S(1)} %copy-done), kind=kLoop, calls=%fused_computation.6 | loop fusion | flops 1835008 | bytes 2097152 | tf_op jit(solution)/shard_map/convert_element_type | solution.py:486
Async XLA Ops:
  0.0 26.5 %copy-start = (bf16[2,8,64,256]{3,2,1,0:T(8,128)(2,1)S(1)}, bf16[2,8,64,256]{3,2,1,0:T(8,128)(2,1)}, u32[]{:S(2)}) copy-start(bf16[2,8,64,256]{3,2,1,0:T(8,128)(2,1)} %param.11) | copy-start | bytes 1572868

commit v2 on v1

--- a/solution.py
+++ b/solution.py
@@ -8,7 +8,10 @@
 from jax.sharding import PartitionSpec as P
 
 WINDOW = 4
-GROUP = 4
+GROUP = 8
+LEAD = 2
+ASK = 4
+PIECES = 2
 BASE = 16
 TILE = 8
 EPS = 1e-06
@@ -153,8 +156,8 @@
     inv = [base_inverse(x, half) for x in spread]
     lc = [jnp.concatenate([s[0][0], s[0][2]], axis=1) for s in stage]
     for mask in masks:
-        mid = [dot(c * mask, expand(x)).astype(BF16) for c, x in zip(lc, inv)]
-        inv = [x - dot(x, expand(z)).astype(BF16) for x, z in zip(inv, mid)]
+        mid = [dot(x, expand(c * mask)).astype(BF16) for c, x in zip(lc, inv)]
+        inv = [x - dot(z, expand(x)).astype(BF16) for x, z in zip(inv, mid)]
     corner = [dot(x[:, :half], s[0][1]).astype(BF16) for s, x in zip(stage, inv)]
     corner = [(-dot(c, x[:, half:])).astype(BF16) for c, x in zip(corner, inv)]
     full = [corner_block(x[:, :half], c, x[:, half:]) for x, c in zip(inv, corner)]
@@ -179,7 +182,7 @@
 
 
 def body(
-    n_seq, hops, per_seq, val_total, group,
+    n_seq, hops, per_seq, val_total, group, lead, ask,
     value_hbm, beta_hbm, decay_hbm, gain_hbm, query_hbm, key_hbm, lengths_hbm, out,
     lengths, value, beta, decay, gain, query, key,
     mask_buf, ones_buf, tri_buf, rate_buf, cum_buf, live_buf, gain_buf,
@@ -202,8 +205,8 @@
 
     def key_load(g):
         return pltpu.make_async_copy(
-            key_hbm.at[pl.ds(base + g * group, group)],
-            key.at[pl.ds(g * group, group)],
+            key_hbm.at[pl.ds(base + g * lead, lead)],
+            key.at[pl.ds(g * lead, lead)],
             key_sem.at[g],
         )
 
@@ -217,9 +220,10 @@
         load(query_hbm.at[mine], query, 5),
         load(lengths_hbm, lengths, 6),
     ]
+    key_load(0).start()
     for copy in loads[:3] + loads[6:]:
         copy.start()
-    for g in range(own // group):
+    for g in range(1, own // lead):
         key_load(g).start()
     for copy in loads[3:6]:
         copy.start()
@@ -248,21 +252,39 @@
         def _():
             depart[...] = jnp.zeros_like(depart)
 
-    loads[0].wait()
-    for p in range(own):
-        val_send[p] = value[peer_base + p].astype(F32)
     loads[1].wait()
     loads[2].wait()
     loads[6].wait()
     position = lax.broadcasted_iota(jnp.int32, (per_seq, tokens), 1)
+    steps = []
     for b in range(2 * own // per_seq):
         live = jnp.where(position < lengths[0, b], 1.0, 0.0)
         rows = pl.ds(b * per_seq, per_seq)
         live_buf[rows, :] = live
         rate_buf[rows, :] = beta[rows, :] * live
-        cum_buf[rows, :] = decay[rows, :] * live
+        steps.append(decay[rows, :] * live)
+    steps = jnp.concatenate(steps, axis=0)
+    high, low = split(steps)
+    rest = (steps - high.astype(F32) - low.astype(F32)).astype(BF16)
+    row = lax.broadcasted_iota(jnp.int32, (tokens, tokens), 0)
+    col = lax.broadcasted_iota(jnp.int32, (tokens, tokens), 1)
+    upto = jnp.where(row <= col, 1.0, 0.0).astype(BF16)
+    cum_buf[...] = dot(high, upto) + dot(low, upto) + dot(rest, upto)
+
+    loads[0].wait()
+    for p in range(own):
+        val_send[p] = value[peer_base + p].astype(F32)
 
     pl.semaphore_wait(barrier, 1 + has_left.astype(jnp.int32) + has_right.astype(jnp.int32))
+
+    def state_copy(p, h):
+        return pltpu.make_async_remote_copy(
+            src_ref=depart.at[p, h],
+            dst_ref=arrive.at[p, h],
+            send_sem=send_sem.at[p, h],
+            recv_sem=recv_sem.at[p, h],
+            device_id={"seq": me + 1},
+        )
 
     def remote(source, target, sent, received, p, where):
         return pltpu.make_async_remote_copy(
@@ -273,9 +295,6 @@
             device_id=where,
         )
 
-    def state_copy(p):
-        return remote(depart, arrive, send_sem, recv_sem, p, {"seq": me + 1})
-
     def value_copy(p):
         return remote(val_send, val_recv, val_send_sem, val_recv_sem, p, {"dim": peer})
 
@@ -285,25 +304,17 @@
     for p in range(own):
         value_copy(p).start()
 
-    row = lax.broadcasted_iota(jnp.int32, (tokens, tokens), 0)
-    col = lax.broadcasted_iota(jnp.int32, (tokens, tokens), 1)
-    upto = jnp.where(row <= col, 1.0, 0.0)
-    cum_buf[...] = jnp.dot(
-        cum_buf[...], upto, precision=lax.Precision.HIGHEST, preferred_element_type=F32
-    )
-    loads[4].wait()
-    row = lax.broadcasted_iota(jnp.int32, (val_width, val_width), 0)
-    col = lax.broadcasted_iota(jnp.int32, (val_width, val_width), 1)
-    gain_col = jnp.sum(jnp.where(row == col, gain[...], 0.0), axis=1, keepdims=True)
-    gain_buf[...] = jnp.broadcast_to(gain_col, gain_buf.shape)
     loads[3].wait()
 
     def row_of(ref, p):
         return ref[pl.ds(base + p, 1), :]
 
-    def key_phase(g, carry):
-        ids = [g * group + u for u in range(group)]
-        key_load(g).wait()
+    piece = val_total // PIECES
+
+    def key_phase(first, size, g, carry):
+        ids = [g * size + u for u in range(size)]
+        for u in range(size // lead):
+            key_load(g * (size // lead) + u).wait()
         items = [(key[p], row_of(rate_buf, p), row_of(cum_buf, p)) for p in ids]
         masks = [mask_buf[index] for index in range(mask_buf.shape[0])]
         tri = [tri_buf[index] for index in range(3)]
@@ -316,68 +327,89 @@
         sides = []
         for p, s, (k, rate, cum) in zip(ids, stage, items):
             val = jnp.concatenate([value[base + p].astype(F32), val_recv[p]], axis=0)
-            kt = k.astype(F32).T
-            sides.append(
-                jnp.concatenate([val * (rate * s[3]), kt * (s[4] * jnp.exp(cum))], axis=0)
-            )
+            side = val * (rate * s[3])
+            if not first:
+                kt = k.astype(F32).T
+                side = jnp.concatenate([side, kt * (s[4] * jnp.exp(cum))], axis=0)
+            sides.append(side)
         solved = solve_terms(stage, full, sides)
         for p, y, (k, rate, cum) in zip(ids, solved, items):
             tail = jnp.exp(cum[:, tokens - 1 :] - cum)
             t_hi, t_lo = split(y * tail)
-            rows = y.shape[0]
-            on_key = dot(jnp.concatenate([t_hi, t_lo], axis=0), k)
-            on_key = on_key[:rows] + on_key[rows:]
-            depart[p, 0] = on_key[:val_total]
-            map_hi[p], map_lo[p] = split(on_key[val_total:])
-            y_hi[p], y_lo[p] = split(y)
-
-        @pl.when(jnp.logical_and(jnp.logical_not(has_left), has_right))
-        def _():
+            on_key = dot(t_hi, k) + dot(t_lo, k)
+            for h in range(PIECES):
+                depart[p, h, 0] = on_key[h * piece : (h + 1) * piece]
+            if not first:
+                map_hi[p], map_lo[p] = split(on_key[val_total:])
+            rows = pl.ds(0, y.shape[0])
+            y_hi[p, rows], y_lo[p, rows] = split(y)
+        if first:
             for p in ids:
-                state_copy(p).start()
-
+                for h in range(PIECES):
+                    state_copy(p, h).start()
         return carry
 
-    lax.fori_loop(0, own // group, key_phase, 0)
+    @pl.when(jnp.logical_not(has_left))
+    def _():
+        lax.fori_loop(0, own // lead, functools.partial(key_phase, True, lead), 0)
+
+    @pl.when(has_left)
+    def _():
+        lax.fori_loop(0, own // group, functools.partial(key_phase, False, group), 0)
+
+    loads[4].wait()
+    row = lax.broadcasted_iota(jnp.int32, (val_width, val_width), 0)
+    col = lax.broadcasted_iota(jnp.int32, (val_width, val_width), 1)
+    gain_col = jnp.sum(jnp.where(row == col, gain[...], 0.0), axis=1, keepdims=True)
+    gain_buf[...] = jnp.broadcast_to(gain_col, gain_buf.shape)
     loads[5].wait()
 
-    def query_phase(p):
-        q, k, cum = query[p], key[p], row_of(cum_buf, p)
-        top = dot_nt(k[:half], q)
-        g22 = dot_nt(k[half:], q[half:])
+    def query_phase(first, size, g, carry):
+        ids = [g * size + u for u in range(size)]
         incl = tri_buf[1]
-        p11 = split(incl * (dec_buf[p, 0] * top[:, :half]))
-        p12 = split(dec_buf[p, 1] * top[:, half:])
-        p22 = split(incl * (dec_buf[p, 2] * g22))
-        p_hi = corner_block(p11[0], p12[0], p22[0])
-        p_lo = corner_block(p11[1], p12[1], p22[1])
-        hi, lo = y_hi[p], y_lo[p]
-        rows = hi.shape[0]
-        both = dot(jnp.concatenate([hi, lo], axis=0), p_hi)
-        on_query = both[:rows] + both[rows:] + dot(hi, p_lo)
-        raw_buf[p] = on_query[:val_total]
-        read = q.astype(F32).T * jnp.exp(cum) - on_query[val_total:]
-        read_hi[p], read_lo[p] = split(read)
-
-    def pass_on(p):
-        state_copy(p).wait_recv()
+        tops = [dot_nt(key[p, :half], query[p]) for p in ids]
+        lows = [dot_nt(key[p, half:], query[p, half:]) for p in ids]
+        parts = []
+        for p, top, low in zip(ids, tops, lows):
+            p11 = split(incl * (dec_buf[p, 0] * top[:, :half]))
+            p12 = split(dec_buf[p, 1] * top[:, half:])
+            p22 = split(incl * (dec_buf[p, 2] * low))
+            parts.append([corner_block(p11[n], p12[n], p22[n]) for n in range(2)])
+        rows = pl.ds(0, val_total if first else val_total + key_width)
+        for p, (p_hi, p_lo) in zip(ids, parts):
+            hi, lo = y_hi[p, rows], y_lo[p, rows]
+            on_query = dot(hi, p_hi) + dot(lo, p_hi) + dot(hi, p_lo)
+            raw_buf[p] = on_query[:val_total]
+            if not first:
+                cum = row_of(cum_buf, p)
+                read = query[p].astype(F32).T * jnp.exp(cum) - on_query[val_total:]
+                read_hi[p], read_lo[p] = split(read)
+        return carry
+
+    def pass_on(p, h):
+        state_copy(p, h).wait_recv()
 
         @pl.when(has_right)
         def _():
             cum = row_of(cum_buf, p)
             decayed = jnp.exp(cum[:, tokens - 1 :])
             if hops == 1:
-                start = arrive[p, 0]
+                start = arrive[p, h, 0]
                 moved = decayed * start - times(start, map_hi[p], map_lo[p])
-                depart[p, 0] = depart[p, 0] + moved
+                depart[p, h, 0] = depart[p, h, 0] + moved
             else:
-                moving = jnp.concatenate([arrive[p, h] for h in range(hops - 1)], axis=0)
+                moving = jnp.concatenate([arrive[p, h, n] for n in range(hops - 1)], axis=0)
                 moved = decayed * moving - times(moving, map_hi[p], map_lo[p])
-                for h in range(hops - 1):
-                    depart[p, h + 1] = moved[h * val_total : (h + 1) * val_total]
-            state_copy(p).start()
-
-        start = functools.reduce(jnp.add, [arrive[p, h] for h in range(hops)])
+                for n in range(hops - 1):
+                    depart[p, h, n + 1] = moved[n * piece : (n + 1) * piece]
+            state_copy(p, h).start()
+
+    def read_out(p):
+        starts = [
+            functools.reduce(jnp.add, [arrive[p, h, n] for n in range(hops)])
+            for h in range(PIECES)
+        ]
+        start = jnp.concatenate(starts, axis=0)
         raw_buf[p] = raw_buf[p] + times(start, read_hi[p], read_lo[p])
 
     def finish(p):
@@ -388,22 +420,50 @@
         out_send[p] = normed[val_width:]
         out_copy(p).start()
 
-    def step(p, carry):
-        query_phase(p)
-
-        @pl.when(has_left)
-        def _():
-            pass_on(p)
-
+    def passing(p, carry):
+        for h in range(PIECES):
+            pass_on(p, h)
+        return carry
+
+    def ending(p, carry):
+        read_out(p)
         finish(p)
         return carry
 
-    lax.fori_loop(0, own, step, 0)
+    def both(p, carry):
+        passing(p, carry)
+        return ending(p, carry)
+
+    def lone(p, carry):
+        finish(p)
+        return carry
+
+    batch = functools.partial(query_phase, False, ask)
+
+    @pl.when(jnp.logical_not(has_left))
+    def _():
+        lax.fori_loop(0, own // ask, functools.partial(query_phase, True, ask), 0)
+        lax.fori_loop(0, own, lone, 0)
+
+    @pl.when(has_left)
+    def _():
+        early = me == 1
+        lax.fori_loop(0, jnp.where(early, own, 0), passing, 0)
+        lax.fori_loop(0, own // ask, batch, 0)
+
+        @pl.when(early)
+        def _():
+            lax.fori_loop(0, own, ending, 0)
+
+        @pl.when(jnp.logical_not(early))
+        def _():
+            lax.fori_loop(0, own, both, 0)
 
     def drain(p, carry):
         @pl.when(has_right)
         def _():
-            state_copy(p).wait_send()
+            for h in range(PIECES):
+                state_copy(p, h).wait_send()
 
         value_copy(p).wait_send()
         out_copy(p).wait_send()
@@ -426,6 +486,8 @@
         own = pairs // n_dim
         half = tokens // 2
         group = max(g for g in range(1, GROUP + 1) if own % g == 0)
+        lead = max(g for g in range(1, LEAD + 1) if group % g == 0)
+        ask = max(g for g in range(1, ASK + 1) if own % g == 0)
         levels = (half // BASE).bit_length() - 1
         vmem = pl.BlockSpec(memory_space=pltpu.VMEM)
         anywhere = pl.BlockSpec(memory_space=pl.ANY)
@@ -435,7 +497,7 @@
         operands = [flat(value), flat(beta), flat(log_decay), norm_gain[None, :]]
         operands += [flat(query), flat(key), lengths.T]
         normed = pl.pallas_call(
-            functools.partial(body, n_seq, hops, heads, val_total, group),
+            functools.partial(body, n_seq, hops, heads, val_total, group, lead, ask),
             out_shape=pltpu.VMEM((pairs, val_width, tokens), F32),
             in_specs=[anywhere] * 7,
             out_specs=vmem,
@@ -462,16 +524,16 @@
                 pltpu.VMEM((own, val_total, tokens), F32),
                 pltpu.VMEM((own, key_width, tokens), BF16),
                 pltpu.VMEM((own, key_width, tokens), BF16),
-                pltpu.VMEM((own, hops, val_total, key_width), F32),
-                pltpu.VMEM((own, hops, val_total, key_width), F32),
+                pltpu.VMEM((own, PIECES, hops, val_total // PIECES, key_width), F32),
+                pltpu.VMEM((own, PIECES, hops, val_total // PIECES, key_width), F32),
                 pltpu.VMEM((own, val_width, tokens), F32),
                 pltpu.VMEM((own, val_width, tokens), F32),
                 pltpu.VMEM((own, val_width, tokens), F32),
                 pltpu.VMEM((own, val_width, tokens), F32),
                 dma((7,)),
-                dma((own // group,)),
-                dma((own,)),
-                dma((own,)),
+                dma((own // lead,)),
+                dma((own, PIECES)),
+                dma((own, PIECES)),
                 dma((own,)),
                 dma((own,)),
                 dma((own,)),

time: 27.8 us -> 24.8 us (0.89)
  Pallas kernels: 26.5 us -> 23.5 us
    pallas_call x1, Pallas kernels: 26.5 us -> 23.5 us  [local(): pl.pallas_call(functools.partial(body, n_seq, hops, heads, val_total, gro...]
where the time goes in v2:
time: 24.8 us; the launch traced here: 24.7 us
  Pallas kernels  23.5 us (95%)
  other arithmetic  1.13 us (5%)
    pallas_call x1, Pallas kernels, local(): pl.pallas_call(functools.partial(body, n_seq, hops, heads, val_total, gro...  23.5 us
    convert_element_type x1, other arithmetic, local(): return gated.astype(BF16)  1.13 us

profile of v2, /device:TPU:31, one launch (start us, length us, event | category | flops | bytes accessed | tf_op | source)
XLA Modules:
  0.0 24.7 jit_solution(8314600289533979237)
XLA Ops:
  0.0 0.0 copy-start
  0.0 23.5 %shard_map.82 = f32[16,64,256]{2,1,0:T(8,128)S(1)} custom-call(bf16[16,64,256]{2,1,0:T(8,128)(2,1)} %bitcast.11, f32[16,256]{1,0:T(8,128)} %bitcast.12, f32[16,256]{1,0:T(8,128)} %bitcast.13, f32[1,64]{1,0:T(1,128)} %bitcast.14, bf16[16,256,128]{2,1,0:T(8,128)(2,1)} %bitcast.9, bf16[16,256,128]{2,1,0:T(8,128)(2,1)} %bitcast.10, s32[1,2]{1,0:T(1,128)} %bitcast.15), custom_call_target="tpu_custom_call" | custom-call | tf_op jit(solution)/shard_map/pallas_call | solution.py:499
  23.5 0.0 copy-done
  23.5 1.1 %fusion.4 = bf16[2,8,64,256]{3,2,1,0:T(8,128)(2,1)} fusion(f32[2,8,64,256]{3,2,1,0:T(8,128)S(1)} %bitcast.8, bf16[2,8,64,256]{3,2,1,0:T(8,128)(2,1)S(1)} %copy-done), kind=kLoop, calls=%fused_computation.6 | loop fusion | flops 1835008 | bytes 2097152 | tf_op jit(solution)/shard_map/convert_element_type | solution.py:548
Async XLA Ops:
  0.0 23.5 %copy-start = (bf16[2,8,64,256]{3,2,1,0:T(8,128)(2,1)S(1)}, bf16[2,8,64,256]{3,2,1,0:T(8,128)(2,1)}, u32[]{:S(2)}) copy-start(bf16[2,8,64,256]{3,2,1,0:T(8,128)(2,1)} %param.11) | copy-start | bytes 1572868

commit v3 on v2

--- a/solution.py
+++ b/solution.py
@@ -121,18 +121,25 @@
     ).astype(BF16)
 
 
+def decays(cum, eye, keep):
+    half = eye.shape[0]
+    cum1, cum2 = cum[:, :half], cum[:, half:]
+    col1 = jnp.sum(eye * cum1, axis=1, keepdims=True)
+    col2 = jnp.sum(eye * cum2, axis=1, keepdims=True)
+    return (
+        jnp.where(keep > 0.0, jnp.exp(cum1 - col1), 0.0),
+        jnp.exp(cum2 - col1),
+        jnp.where(keep > 0.0, jnp.exp(cum2 - col2), 0.0),
+    )
+
+
 def key_terms(items, masks, ones, tri):
     strict, _, eye = tri
     tokens = items[0][0].shape[0]
     half = tokens // 2
     stage = []
     for k, rate, cum in items:
-        cum1, cum2 = cum[:, :half], cum[:, half:]
-        col1 = jnp.sum(eye * cum1, axis=1, keepdims=True)
-        col2 = jnp.sum(eye * cum2, axis=1, keepdims=True)
-        d11 = jnp.exp(jnp.minimum(cum1 - col1, 0.0))
-        d12 = jnp.exp(jnp.minimum(cum2 - col1, 0.0))
-        d22 = jnp.exp(jnp.minimum(cum2 - col2, 0.0))
+        d11, d12, d22 = decays(cum, eye, strict)
         top = dot_nt(k[:half], k)
         g22 = dot_nt(k[half:], k[half:])
         norm = jnp.concatenate(
@@ -144,14 +151,14 @@
         )
         r = lax.rsqrt(norm + EPS)
         w = rate * (r * r)
-        l11 = strict * (d11 * top[:, :half]) * w[:, :half]
+        l11 = d11 * top[:, :half] * w[:, :half]
         l12 = d12 * top[:, half:] * w[:, half:]
-        l22 = strict * (d22 * g22) * w[:, half:]
+        l22 = d22 * g22 * w[:, half:]
         packed = jnp.concatenate([l11, l22], axis=1)
-        pair = [split(x) for x in (l11, l12, l22)]
+        pair = [split(x) for x in (l11 + eye, l12, l22 + eye)]
         l_hi = [x[0] for x in pair]
         l_lo = [x[1] for x in pair]
-        stage.append((l_hi, l_lo, packed, r, w, (d11, d12, d22)))
+        stage.append((l_hi, l_lo, packed, r, w))
     spread = [dot(base_rows(s[2]), ones) for s in stage]
     inv = [base_inverse(x, half) for x in spread]
     lc = [jnp.concatenate([s[0][0], s[0][2]], axis=1) for s in stage]
@@ -168,7 +175,7 @@
     lower = [(corner_block(*s[0]), corner_block(*s[1])) for s in stage]
     first = [dot(rhs.astype(BF16), x).astype(BF16) for rhs, x in zip(sides, full)]
     rest = [
-        rhs - y.astype(F32) - (dot(y, l[0]) + dot(y, l[1]))
+        rhs - (dot(y, l[0]) + dot(y, l[1]))
         for rhs, y, l in zip(sides, first, lower)
     ]
     return [y.astype(F32) + dot(r.astype(BF16), x) for y, r, x in zip(first, rest, full)]
@@ -186,7 +193,7 @@
     value_hbm, beta_hbm, decay_hbm, gain_hbm, query_hbm, key_hbm, lengths_hbm, out,
     lengths, value, beta, decay, gain, query, key,
     mask_buf, ones_buf, tri_buf, rate_buf, cum_buf, live_buf, gain_buf,
-    dec_buf, y_hi, y_lo, map_hi, map_lo, raw_buf, read_hi, read_lo,
+    y_buf, map_hi, map_lo, raw_buf, read_hi, read_lo,
     arrive, depart, val_send, val_recv, out_send, out_recv,
     load_sem, key_sem, send_sem, recv_sem,
     val_send_sem, val_recv_sem, out_send_sem, out_recv_sem,
@@ -310,6 +317,7 @@
         return ref[pl.ds(base + p, 1), :]
 
     piece = val_total // PIECES
+    assert piece == val_width
 
     def key_phase(first, size, g, carry):
         ids = [g * size + u for u in range(size)]
@@ -319,34 +327,43 @@
         masks = [mask_buf[index] for index in range(mask_buf.shape[0])]
         tri = [tri_buf[index] for index in range(3)]
         stage, full = key_terms(items, masks, ones_buf[...], tri)
-        for p, s in zip(ids, stage):
-            for index, block in enumerate(s[5]):
-                dec_buf[p, index] = block
-        for p in ids:
-            value_copy(p).wait_recv()
-        sides = []
-        for p, s, (k, rate, cum) in zip(ids, stage, items):
-            val = jnp.concatenate([value[base + p].astype(F32), val_recv[p]], axis=0)
-            side = val * (rate * s[3])
-            if not first:
-                kt = k.astype(F32).T
-                side = jnp.concatenate([side, kt * (s[4] * jnp.exp(cum))], axis=0)
-            sides.append(side)
-        solved = solve_terms(stage, full, sides)
-        for p, y, (k, rate, cum) in zip(ids, solved, items):
-            tail = jnp.exp(cum[:, tokens - 1 :] - cum)
-            t_hi, t_lo = split(y * tail)
-            on_key = dot(t_hi, k) + dot(t_lo, k)
+        if first:
+            tails = [jnp.exp(cum[:, tokens - 1 :] - cum) for k, rate, cum in items]
             for h in range(PIECES):
-                depart[p, h, 0] = on_key[h * piece : (h + 1) * piece]
-            if not first:
-                map_hi[p], map_lo[p] = split(on_key[val_total:])
-            rows = pl.ds(0, y.shape[0])
-            y_hi[p, rows], y_lo[p, rows] = split(y)
-        if first:
+                if h > 0:
+                    for p in ids:
+                        value_copy(p).wait_recv()
+                parts = [val_recv[p] if h else value[base + p].astype(F32) for p in ids]
+                sides = [v * (rate * s[3]) for v, s, (k, rate, cum) in zip(parts, stage, items)]
+                solved = solve_terms(stage, full, sides)
+                for p, y, tail, (k, rate, cum) in zip(ids, solved, tails, items):
+                    t_hi, t_lo = split(y * tail)
+                    depart[p, h, 0] = dot(t_hi, k) + dot(t_lo, k)
+                for p in ids:
+                    state_copy(p, h).start()
+                for p, y in zip(ids, solved):
+                    y_buf[p, pl.ds(h * piece, piece)] = y
+        else:
             for p in ids:
+                value_copy(p).wait_recv()
+            sides = []
+            for p, s, (k, rate, cum) in zip(ids, stage, items):
+                val = jnp.concatenate([value[base + p].astype(F32), val_recv[p]], axis=0)
+                side = val * (rate * s[3])
+                if not first:
+                    kt = k.astype(F32).T
+                    side = jnp.concatenate([side, kt * (s[4] * jnp.exp(cum))], axis=0)
+                sides.append(side)
+            solved = solve_terms(stage, full, sides)
+            for p, y, (k, rate, cum) in zip(ids, solved, items):
+                tail = jnp.exp(cum[:, tokens - 1 :] - cum)
+                t_hi, t_lo = split(y * tail)
+                on_key = dot(t_hi, k) + dot(t_lo, k)
                 for h in range(PIECES):
-                    state_copy(p, h).start()
+                    depart[p, h, 0] = on_key[h * piece : (h + 1) * piece]
+                if not first:
+                    map_hi[p], map_lo[p] = split(on_key[val_total:])
+                y_buf[p, pl.ds(0, y.shape[0])] = y
         return carry
 
     @pl.when(jnp.logical_not(has_left))
@@ -357,6 +374,8 @@
     def _():
         lax.fori_loop(0, own // group, functools.partial(key_phase, False, group), 0)
 
+    for p in range(own):
+        value_copy(p).wait_send()
     loads[4].wait()
     row = lax.broadcasted_iota(jnp.int32, (val_width, val_width), 0)
     col = lax.broadcasted_iota(jnp.int32, (val_width, val_width), 1)
@@ -371,13 +390,14 @@
         lows = [dot_nt(key[p, half:], query[p, half:]) for p in ids]
         parts = []
         for p, top, low in zip(ids, tops, lows):
-            p11 = split(incl * (dec_buf[p, 0] * top[:, :half]))
-            p12 = split(dec_buf[p, 1] * top[:, half:])
-            p22 = split(incl * (dec_buf[p, 2] * low))
+            d11, d12, d22 = decays(row_of(cum_buf, p), tri_buf[2], incl)
+            p11 = split(d11 * top[:, :half])
+            p12 = split(d12 * top[:, half:])
+            p22 = split(d22 * low)
             parts.append([corner_block(p11[n], p12[n], p22[n]) for n in range(2)])
         rows = pl.ds(0, val_total if first else val_total + key_width)
         for p, (p_hi, p_lo) in zip(ids, parts):
-            hi, lo = y_hi[p, rows], y_lo[p, rows]
+            hi, lo = split(y_buf[p, rows])
             on_query = dot(hi, p_hi) + dot(lo, p_hi) + dot(hi, p_lo)
             raw_buf[p] = on_query[:val_total]
             if not first:
@@ -459,19 +479,17 @@
         def _():
             lax.fori_loop(0, own, both, 0)
 
-    def drain(p, carry):
-        @pl.when(has_right)
-        def _():
+    for p in range(own):
+        out_copy(p).wait_recv()
+        out[peer_base + p] = out_recv[p] * gain_buf[...]
+    for p in range(own):
+        out_copy(p).wait_send()
+
+    @pl.when(has_right)
+    def _():
+        for p in range(own):
             for h in range(PIECES):
                 state_copy(p, h).wait_send()
-
-        value_copy(p).wait_send()
-        out_copy(p).wait_send()
-        out_copy(p).wait_recv()
-        out[peer_base + p] = out_recv[p] * gain_buf[...]
-        return carry
-
-    lax.fori_loop(0, own, drain, 0)
 
 
 def solution(mesh):
@@ -516,9 +534,7 @@
                 pltpu.VMEM((pairs, tokens), F32),
                 pltpu.VMEM((pairs, tokens), F32),
                 pltpu.VMEM((val_width, tokens), F32),
-                pltpu.VMEM((own, 3, half, half), F32),
-                pltpu.VMEM((own, val_total + key_width, tokens), BF16),
-                pltpu.VMEM((own, val_total + key_width, tokens), BF16),
+                pltpu.VMEM((own, val_total + key_width, tokens), F32),
                 pltpu.VMEM((own, key_width, key_width), BF16),
                 pltpu.VMEM((own, key_width, key_width), BF16),
                 pltpu.VMEM((own, val_total, tokens), F32),

time: 24.8 us -> 24.8 us (level)
  no operation moved by 1% of the time
where the time goes in v3:
time: 24.8 us; the launch traced here: 24.7 us
  Pallas kernels  23.5 us (95%)
  other arithmetic  1.13 us (5%)
    pallas_call x1, Pallas kernels, local(): pl.pallas_call(functools.partial(body, n_seq, hops, heads, val_total, gro...  23.5 us
    convert_element_type x1, other arithmetic, local(): return gated.astype(BF16)  1.13 us

profile of v3, /device:TPU:31, one launch (start us, length us, event | category | flops | bytes accessed | tf_op | source)
XLA Modules:
  0.0 24.7 jit_solution(11837019916154446969)
XLA Ops:
  0.0 0.0 copy-start
  0.0 23.5 %shard_map.82 = f32[16,64,256]{2,1,0:T(8,128)S(1)} custom-call(bf16[16,64,256]{2,1,0:T(8,128)(2,1)} %bitcast.11, f32[16,256]{1,0:T(8,128)} %bitcast.12, f32[16,256]{1,0:T(8,128)} %bitcast.13, f32[1,64]{1,0:T(1,128)} %bitcast.14, bf16[16,256,128]{2,1,0:T(8,128)(2,1)} %bitcast.9, bf16[16,256,128]{2,1,0:T(8,128)(2,1)} %bitcast.10, s32[1,2]{1,0:T(1,128)} %bitcast.15), custom_call_target="tpu_custom_call" | custom-call | tf_op jit(solution)/shard_map/pallas_call | solution.py:517
  23.5 0.0 copy-done
  23.5 1.1 %fusion.4 = bf16[2,8,64,256]{3,2,1,0:T(8,128)(2,1)} fusion(f32[2,8,64,256]{3,2,1,0:T(8,128)S(1)} %bitcast.8, bf16[2,8,64,256]{3,2,1,0:T(8,128)(2,1)S(1)} %copy-done), kind=kLoop, calls=%fused_computation.6 | loop fusion | flops 1835008 | bytes 2097152 | tf_op jit(solution)/shard_map/convert_element_type | solution.py:564
Async XLA Ops:
  0.0 23.5 %copy-start = (bf16[2,8,64,256]{3,2,1,0:T(8,128)(2,1)S(1)}, bf16[2,8,64,256]{3,2,1,0:T(8,128)(2,1)}, u32[]{:S(2)}) copy-start(bf16[2,8,64,256]{3,2,1,0:T(8,128)(2,1)} %param.11) | copy-start | bytes 1572868
